TPU v7x, 512 devices: a 8x2x16 block of a 8x8x16 slice. The times are simulated.
512 devices in a mesh: subj: 2 (over y), row: 16 (over x, core), col: 16 (over z).
Axes of the slice: x: 8, y: 2, z: 16, core: 2. Of those that a mesh axis runs over, the one named last changes fastest.
The devices are a block of a 8x8x16 slice.
Arguments:
- series: float32 [800, 65536], P(None, ('subj', 'row', 'col')), parts along dimension 1, as said below
- keep_mask: int32 [512, 256], P(('subj', 'row'), 'col'), parts along dimension 0, may hold values from 0 to 1, as said below
- row_owner: int32 [512], P('subj'), parts along dimension 0, may hold values from 0 to 15, as said below
Outputs:
- owned_tiles: bfloat16 [32, 16, 96, 128, 128], P(('subj', 'row'), 'col'), parts along dimension 0
- owned_ids: int32 [32, 16, 96], P(('subj', 'row'), 'col'), parts along dimension 0
There are 2 independent parts, one for each index of `subj`. A program takes and returns all parts, laid end to end along the dimension named above; each array names one. Nothing has to cross between parts.
Inputs may be any that keep to these rules, and one draw needn't show every extreme that they name: Each voxel's series varies over time. `keep_mask`: of the 16 tiles that one tile row has in one column block, at most 6 are kept; in every draw one owner keeps exactly 6 in each of its tile rows in some column block. `row_owner`: the 16 tile rows of a row block have 16 different owners, and every owner holds 16 tile rows, from 16 different row blocks.
All inputs are finite; a program needn't handle non-finite values.
Results may differ from a plain program's by a relative error of at most 0.0042.
Values may be sent and summed in bfloat16 or wider, within the bound.
No kernel may reach another device: no remote copies, remote signals or barrier semaphores. Data moves between devices by JAX's collectives and lax.ppermute only.
A program may use at most 64 MiB of HBM per device.

v0:
```python
import jax
import jax.numpy as jnp
from jax import lax
from jax.sharding import PartitionSpec as P

TILE = 128
epsilon = 1e-05


def compact(flat_tiles, flat_ids, capacity):
    is_valid = (flat_ids >= 0).astype(jnp.int32)
    running = jnp.cumsum(is_valid)
    slot_index = jnp.arange(capacity, dtype=jnp.int32)
    position = jnp.arange(flat_ids.shape[0], dtype=jnp.int32)
    slot_hit = (is_valid[None, :] == 1) & (running[None, :] == slot_index[:, None] + 1)
    picked = jnp.sum(jnp.where(slot_hit, position[None, :], 0), axis=1)
    present = running[-1] > slot_index
    chosen = jnp.take(flat_tiles, picked, axis=0)
    slot_tiles = jnp.where(present[:, None, None], chosen, jnp.zeros_like(chosen))
    slot_ids = jnp.where(present, jnp.take(flat_ids, picked), -1).astype(jnp.int32)
    return (slot_tiles, slot_ids)


def shards(series, keep_mask, row_owner):
    frames = series.shape[0]
    average = jnp.mean(series, axis=0, keepdims=True)
    centred = series - average
    spread = jnp.mean(centred * centred, axis=0, keepdims=True)
    scored = (centred * lax.rsqrt(spread + epsilon)).astype(jnp.bfloat16)
    row_block = lax.all_gather(scored, "col", axis=1, tiled=True)
    product = lax.dot_general(
        row_block,
        lax.all_gather(scored, "row", axis=1, tiled=True),
        (((0,), (0,)), ((), ())),
        preferred_element_type=jnp.float32,
    )
    tile_grid = (product * (1.0 / frames)).astype(jnp.bfloat16)
    row_count, col_count = keep_mask.shape
    tile_grid = tile_grid.reshape(row_count, TILE, col_count, TILE).transpose(0, 2, 1, 3)
    row_devices = lax.axis_size("row")
    col_devices = lax.axis_size("col")
    row_index = lax.axis_index("row")
    col_index = lax.axis_index("col")
    total_cols = col_count * col_devices
    slot_limit = max(2, 3 * col_count // 8)
    capacity = row_count * slot_limit
    local_owner = lax.dynamic_slice_in_dim(row_owner, row_index * row_count, row_count)
    targets = jnp.arange(row_devices, dtype=jnp.int32)
    owns_row = local_owner[None, :] == targets[:, None]
    has_row = jnp.any(owns_row, axis=1)
    row_of = jnp.sum(
        jnp.where(owns_row, jnp.arange(row_count, dtype=jnp.int32)[None, :], 0), axis=1
    )
    keep_flags = jnp.where(has_row[:, None], jnp.take(keep_mask, row_of, axis=0), 0)
    global_row = row_index * row_count + row_of
    first_col = col_index * col_count
    running = jnp.cumsum(keep_flags, axis=1)
    slot_index = jnp.arange(slot_limit, dtype=jnp.int32)
    slot_hit = (keep_flags[:, None, :] == 1) & (
        running[:, None, :] == slot_index[None, :, None] + 1
    )
    picked = jnp.sum(
        jnp.where(slot_hit, jnp.arange(col_count, dtype=jnp.int32)[None, None, :], 0), axis=2
    )
    present = running[:, -1:] > slot_index[None, :]
    chosen = tile_grid[row_of[:, None], picked]
    outgoing = jnp.where(present[:, :, None, None], chosen, jnp.zeros_like(chosen))
    out_ids = jnp.where(present, global_row[:, None] * total_cols + first_col + picked, -1)
    incoming, in_ids = (
        lax.all_to_all(outgoing, "row", split_axis=0, concat_axis=0, tiled=True),
        lax.all_to_all(out_ids, "row", split_axis=0, concat_axis=0, tiled=True),
    )
    flat_tiles = incoming.reshape(-1, TILE, TILE)
    flat_ids = in_ids.reshape(-1)
    slot_tiles, slot_ids = compact(flat_tiles, flat_ids, capacity)
    return (slot_tiles.reshape(1, 1, capacity, TILE, TILE), slot_ids.reshape(1, 1, capacity))


def solution(mesh):
    in_specs = (P(None, ("subj", "row", "col")), P(("subj", "row"), "col"), P("subj"))
    out_specs = (P(("subj", "row"), "col", None, None, None), P(("subj", "row"), "col", None))
    return jax.shard_map(shards, mesh=mesh, in_specs=in_specs, out_specs=out_specs, check_vma=False)
```

profile of v0, /device:TPU:65, one launch (start us, length us, event | category | flops | bytes accessed | tf_op | source)
XLA Modules:
  0.0 313.3 jit_solution(12894685114126903149)
XLA Ops:
  7.2 0.0 copy-start
  7.2 0.1 all-gather.3.cloned.1.call-start
  7.3 1.1 reduce_sum.60
  8.4 1.1 multiply_reduce_fusion
  9.5 1.7 multiply_convert_fusion.1
  11.3 0.1 all-gather.3.cloned.1.call-update
  11.3 0.1 all-gather.5.cloned.1.call-start
  11.4 0.7 all-gather.5.cloned.1.call-update
  12.1 0.8 dynamic_slice.3
  12.9 0.1 select_reduce_fusion.2
  13.0 0.0 copy-done
  13.0 0.6 gather_fusion
  13.6 0.1 fusion.3
  13.7 0.1 broadcast_compare_fusion
  13.8 0.2 reduce_window_sum.18
  14.0 0.2 slice_reduce_fusion
  14.2 0.3 select_reduce_fusion.1
  14.4 0.7 copy.18
  15.1 44.6 %all-to-all-start = ((s32[16,1,6]{2,1,0:T(1,128)}), s32[16,1,6]{2,1,0:T(1,128)S(1)}, u32[]{:S(2)}, u32[]{:S(2)}) async-start(s32[16,1,6]{2,1,0:T(1,128)} %copy.18), calls=%async_computation | async-start | bytes 16384 | tf_op jit(solution)/shard_map/all_to_all | solution.py:71
  59.8 0.1 copy.21
  59.9 0.1 reshape.311
  59.9 0.1 iota_compare_fusion
  60.0 64.0 %all-gather.3.cloned.1.call-done = bf16[800,2048]{1,0:T(8,128)(2,1)} async-done(((bf16[800,128]{1,0:T(8,128)(2,1)}), bf16[800,2048]{1,0:T(8,128)(2,1)}) %all-gather.3.cloned.1.call-update) | async-done | bytes 3276816 | tf_op jit(solution)/shard_map/all_gather | solution.py:30
  124.0 61.5 %all-gather.5.cloned.1.call-done = bf16[800,2048]{1,0:T(8,128)(2,1)} async-done(((bf16[800,128]{1,0:T(8,128)(2,1)}), bf16[800,2048]{1,0:T(8,128)(2,1)}) %all-gather.5.cloned.1.call-update) | async-done | bytes 3276816 | tf_op jit(solution)/shard_map/all_gather | solution.py:33
  185.5 13.6 %fusion = bf16[256,8,16,128]{3,1,2,0:T(8,128)(2,1)} fusion(bf16[800,2048]{1,0:T(8,128)(2,1)} %all-gather.3.cloned.1.call-done, bf16[800,2048]{1,0:T(8,128)(2,1)} %all-gather.5.cloned.1.call-done), kind=kOutput, calls=%fused_computation.6 | convolution fusion | flops 6719275008 | bytes 14942208 | tf_op jit(solution)/shard_map/dot_general | solution.py:31
  199.2 9.7 %copy.22 = bf16[256,8,16,128]{3,2,1,0:T(8,128)(2,1)} copy(bf16[256,8,16,128]{3,1,2,0:T(8,128)(2,1)} %fusion) | data formatting | bytes 16777216
  208.9 9.1 %copy.24 = bf16[16,128,16,128]{3,1,2,0:T(8,128)(2,1)} copy(bf16[16,128,16,128]{3,2,1,0:T(8,128)(2,1)} %bitcast.36) | data formatting | bytes 16777216 | tf_op jit(solution)/shard_map/reshape | solution.py:39
  218.0 4.9 %gather_fusion.1 = bf16[96,128,128]{2,1,0:T(8,128)(2,1)S(1)} fusion(bf16[16,16,128,128]{3,2,1,0:T(8,128)(2,1)} %bitcast.37, s32[96]{0:T(128)S(1)} %reshape.311), kind=kCustom, calls=%fused_computation.1 | custom fusion | bytes 6292224 | tf_op jit(solution)/shard_map/gather | solution.py:66
  223.0 1.9 broadcast_select_fusion
  224.9 0.0 all-to-all-done
  224.9 4.5 %all-to-all-start.1 = ((bf16[16,6,128,128]{3,2,1,0:T(8,128)(2,1)}), bf16[16,6,128,128]{3,2,1,0:T(8,128)(2,1)S(1)}, u32[]{:S(2)}, u32[]{:S(2)}) async-start(bf16[16,6,128,128]{3,2,1,0:T(8,128)(2,1)} %broadcast_select_fusion), calls=%async_computation.1 | async-start | bytes 6291456 | tf_op jit(solution)/shard_map/all_to_all | solution.py:70
  229.4 0.5 broadcast.364
  229.9 0.7 fusion.11
  230.6 0.1 reshape.333
  230.7 0.1 reduce-window.4
  230.8 0.1 reduce.3
  230.9 0.6 slice.21
  231.5 0.1 reshape.299
  231.6 0.2 select_reduce_fusion
  231.8 1.2 gather_fusion.3
  233.1 0.7 compare_and_fusion
  233.8 1.2 compare_select_fusion.6
  235.0 65.3 %all-to-all-done.1 = bf16[16,6,128,128]{3,2,1,0:T(8,128)(2,1)S(1)} async-done(((bf16[16,6,128,128]{3,2,1,0:T(8,128)(2,1)}), bf16[16,6,128,128]{3,2,1,0:T(8,128)(2,1)S(1)}, u32[]{:S(2)}, u32[]{:S(2)}) %all-to-all-start.1) | async-done | bytes 3145760 | tf_op jit(solution)/shard_map/all_to_all | solution.py:70
  300.3 2.7 gather_fusion.2
  303.0 3.4 %fusion.1 = bf16[1,1,96,128,128]{4,3,2,1,0:T(8,128)(2,1)} fusion(bf16[96,128,128]{2,1,0:T(8,128)(2,1)} %gather_fusion.2, pred[96]{0:T(512)(128)(4,1)S(1)} %get-tuple-element.8, pred[96]{0:T(512)(128)(4,1)S(1)} %get-tuple-element.9), kind=kLoop, calls=%fused_computation.8 | loop fusion | flops 3145728 | bytes 6291648 | tf_op jit(solution)/shard_map/jit(_where)/select_n | solution.py:19
  (13 shorter events, 0.1 us)
Async XLA Ops:
  7.2 5.9 %copy-start = (s32[16,16]{1,0:T(8,128)S(1)}, s32[16,16]{1,0:T(8,128)}, u32[]{:S(2)}) copy-start(s32[16,16]{1,0:T(8,128)} %param.4) | copy-start | bytes 3076
  7.2 116.8 %all-gather.3.cloned.1.call-start = ((), (), s32[]{:S(2)}) async-start(), calls=%async_computation.2 | async-start | bytes 3481600 | tf_op jit(solution)/shard_map/all_gather | solution.py:30
  11.3 174.2 %all-gather.5.cloned.1.call-start = ((), (), s32[]{:S(2)}) async-start(), calls=%async_computation.3 | async-start | bytes 3481600 | tf_op jit(solution)/shard_map/all_gather | solution.py:33
  15.1 209.8 %all-to-all-start = ((s32[16,1,6]{2,1,0:T(1,128)}), s32[16,1,6]{2,1,0:T(1,128)S(1)}, u32[]{:S(2)}, u32[]{:S(2)}) async-start(s32[16,1,6]{2,1,0:T(1,128)} %copy.18), calls=%async_computation | async-start | bytes 16384 | tf_op jit(solution)/shard_map/all_to_all | solution.py:71
  224.9 75.4 %all-to-all-start.1 = ((bf16[16,6,128,128]{3,2,1,0:T(8,128)(2,1)}), bf16[16,6,128,128]{3,2,1,0:T(8,128)(2,1)S(1)}, u32[]{:S(2)}, u32[]{:S(2)}) async-start(bf16[16,6,128,128]{3,2,1,0:T(8,128)(2,1)} %broadcast_select_fusion), calls=%async_computation.1 | async-start | bytes 6291456 | tf_op jit(solution)/shard_map/all_to_all | solution.py:70
Sparse Core Ops, SparseCore 0:
  11.4 112.5 all-gather.2
  126.6 58.8 all-gather.4
where the time goes:
time: 314 us; the launch traced here: 313 us
  waiting for transfers between devices  192 us (61%)
  starting transfers between devices  49.2 us (16%)
  local copies, waits for them, and re-layouts  31.4 us (10%)
  between operations  14.2 us (5%)
  matrix products  13.6 us (4%)
  other arithmetic  13.2 us (4%)
    all_to_all x1, waiting for transfers between devices, shards(): lax.all_to_all(outgoing, 'row', split_axis=0, concat_axis=0, tiled=True)  65.3 us
    all_gather x1, waiting for transfers between devices, shards(): row_block = lax.all_gather(scored, 'col', axis=1, tiled=True)  64 us
    all_gather x1, waiting for transfers between devices, shards(): lax.all_gather(scored, 'row', axis=1, tiled=True)  61.5 us
    all_to_all x1, starting transfers between devices, shards(): lax.all_to_all(out_ids, 'row', split_axis=0, concat_axis=0, tiled=True)  44.6 us
    dot_general x1, matrix products, shards(): lax.dot_general(row_block, lax.all_gather(scored, 'row', axis=1, tiled=Tr...  13.6 us
    unnamed x3, local copies, waits for them, and re-layouts  9.76 us
    reshape x1, local copies, waits for them, and re-layouts, shards(): tile_grid.reshape(row_count, TILE, col_count, TILE).transpose(0, 2, 1, 3)  9.11 us
  transfers between devices with their start and end apart: 4, of which 3 were waited for; matrix products, arithmetic and copies ran while one was open for 15% of the time, Pallas kernels for 0%

commit v1 on v0

--- a/solution.py
+++ b/solution.py
@@ -5,6 +5,23 @@
 
 TILE = 128
 epsilon = 1e-05
+
+
+def joined_along(pieces, dim):
+    shape = list(pieces.shape[1:])
+    shape[dim] *= pieces.shape[0]
+    return jnp.moveaxis(pieces, 0, dim).reshape(shape)
+
+
+def collect(x, axis, dim):
+    size = lax.axis_size(axis)
+    ahead = [(i, (i + 1) % size) for i in range(size)]
+    blocks = [x]
+    while len(blocks) < size:
+        blocks.append(lax.ppermute(blocks[-1], axis, ahead))
+    index = lax.axis_index(axis)
+    blocks = jnp.stack(blocks)[(index - jnp.arange(size)) % size]
+    return joined_along(blocks, dim)
 
 
 def compact(flat_tiles, flat_ids, capacity):
@@ -30,7 +47,7 @@
     row_block = lax.all_gather(scored, "col", axis=1, tiled=True)
     product = lax.dot_general(
         row_block,
-        lax.all_gather(scored, "row", axis=1, tiled=True),
+        collect(scored, "row", 1),
         (((0,), (0,)), ((), ())),
         preferred_element_type=jnp.float32,
     )

time: 314 us -> 284 us (0.904)
  waiting for transfers between devices: 192 us -> 138 us
  starting transfers between devices: 49.2 us -> 69.7 us
    ppermute x0 -> x15, waiting for transfers between devices: none -> 72.4 us  [collect(): blocks.append(lax.ppermute(blocks[-1], axis, ahead))]
    all_gather x1, waiting for transfers between devices: 64 us -> 0.01 us  [shards(): row_block = lax.all_gather(scored, 'col', axis=1, tiled=True)]
    all_gather x1 -> x0, waiting for transfers between devices: 61.5 us -> none  [shards(): lax.all_gather(scored, 'row', axis=1, tiled=True)]
    ppermute x0 -> x15, starting transfers between devices: none -> 14.4 us  [collect(): blocks.append(lax.ppermute(blocks[-1], axis, ahead))]
    all_to_all x1, starting transfers between devices: 4.46 us -> 12.3 us  [shards(): lax.all_to_all(outgoing, 'row', split_axis=0, concat_axis=0, tiled=True)]
    unnamed x3 -> x17, local copies, waits for them, and re-layouts: 9.76 us -> 10.1 us
  transfers between devices with their start and end apart: 4 -> 18, of which waited for: 3 -> 15; matrix products, arithmetic and copies ran while one was open for 15% -> 18% of each run, Pallas kernels for 0% -> 0%
where the time goes in v1:
time: 284 us; the launch traced here: 283 us
  waiting for transfers between devices  138 us (49%)
  starting transfers between devices  69.7 us (25%)
  local copies, waits for them, and re-layouts  34.5 us (12%)
  between operations  14.3 us (5%)
  matrix products  13.6 us (5%)
  other arithmetic  13.3 us (5%)
    ppermute x15, waiting for transfers between devices, collect(): blocks.append(lax.ppermute(blocks[-1], axis, ahead))  72.4 us
    all_to_all x1, waiting for transfers between devices, shards(): lax.all_to_all(outgoing, 'row', split_axis=0, concat_axis=0, tiled=True)  65.3 us
    all_to_all x1, starting transfers between devices, shards(): lax.all_to_all(out_ids, 'row', split_axis=0, concat_axis=0, tiled=True)  43 us
    ppermute x15, starting transfers between devices, collect(): blocks.append(lax.ppermute(blocks[-1], axis, ahead))  14.4 us
    dot_general x1, matrix products, shards(): lax.dot_general(row_block, collect(scored, 'row', 1), (((0,), (0,)), ((),...  13.6 us
    all_to_all x1, starting transfers between devices, shards(): lax.all_to_all(outgoing, 'row', split_axis=0, concat_axis=0, tiled=True)  12.3 us
    unnamed x17, local copies, waits for them, and re-layouts  10.1 us
    reshape x1, local copies, waits for them, and re-layouts, shards(): tile_grid.reshape(row_count, TILE, col_count, TILE).transpose(0, 2, 1, 3)  9.11 us
  transfers between devices with their start and end apart: 18, of which 15 were waited for; matrix products, arithmetic and copies ran while one was open for 18% of the time, Pallas kernels for 0%

profile of v1, /device:TPU:65, one launch (start us, length us, event | category | flops | bytes accessed | tf_op | source)
XLA Modules:
  0.0 283.2 jit_solution(18172492064835712832)
XLA Ops:
  7.3 1.1 reduce_sum.60
  8.4 1.1 multiply_reduce_fusion
  9.5 1.7 bitcast_dynamic-update-slice_fusion.15
  11.3 2.7 collective-permute-start
  14.0 0.8 dynamic_slice.3
  14.9 0.6 gather_fusion
  15.7 0.2 reduce_window_sum.18
  15.9 0.2 slice_reduce_fusion
  16.0 0.3 select_reduce_fusion.1
  16.3 0.7 copy.20
  17.0 43.0 %all-to-all-start = ((s32[16,1,6]{2,1,0:T(1,128)}), s32[16,1,6]{2,1,0:T(1,128)S(1)}, u32[]{:S(2)}, u32[]{:S(2)}) async-start(s32[16,1,6]{2,1,0:T(1,128)} %copy.20), calls=%async_computation | async-start | bytes 16384 | tf_op jit(solution)/shard_map/all_to_all | solution.py:88
  60.3 1.6 collective-permute-start.1
  62.0 2.7 collective-permute-done.1
  64.8 2.5 collective-permute-start.2
  67.3 2.7 collective-permute-done.2
  70.0 2.5 collective-permute-start.3
  72.5 2.7 collective-permute-done.3
  75.1 2.5 collective-permute-start.4
  77.6 3.3 %collective-permute-done.4 = bf16[800,128]{1,0:T(8,128)(2,1)S(1)} collective-permute-done((bf16[800,128]{1,0:T(8,128)(2,1)S(1)}, bf16[800,128]{1,0:T(8,128)(2,1)S(1)}, u32[]{:S(2)}, u32[]{:S(2)}) %collective-permute-start.4) | collective-permute-done | bytes 204832 | tf_op jit(solution)/shard_map/ppermute | solution.py:21
  80.9 1.9 collective-permute-start.5
  82.8 4.5 %collective-permute-done.5 = bf16[800,128]{1,0:T(8,128)(2,1)S(1)} collective-permute-done((bf16[800,128]{1,0:T(8,128)(2,1)S(1)}, bf16[800,128]{1,0:T(8,128)(2,1)S(1)}, u32[]{:S(2)}, u32[]{:S(2)}) %collective-permute-start.5) | collective-permute-done | bytes 204832 | tf_op jit(solution)/shard_map/ppermute | solution.py:21
  87.3 0.7 collective-permute-start.6
  88.0 5.7 %collective-permute-done.6 = bf16[800,128]{1,0:T(8,128)(2,1)S(1)} collective-permute-done((bf16[800,128]{1,0:T(8,128)(2,1)S(1)}, bf16[800,128]{1,0:T(8,128)(2,1)S(1)}, u32[]{:S(2)}, u32[]{:S(2)}) %collective-permute-start.6) | collective-permute-done | bytes 204832 | tf_op jit(solution)/shard_map/ppermute | solution.py:21
  93.7 6.4 %collective-permute-done.7 = bf16[800,128]{1,0:T(8,128)(2,1)S(1)} collective-permute-done((bf16[800,128]{1,0:T(8,128)(2,1)S(1)}, bf16[800,128]{1,0:T(8,128)(2,1)S(1)}, u32[]{:S(2)}, u32[]{:S(2)}) %collective-permute-start.7) | collective-permute-done | bytes 204832 | tf_op jit(solution)/shard_map/ppermute | solution.py:21
  100.1 6.4 %collective-permute-done.8 = bf16[800,128]{1,0:T(8,128)(2,1)S(1)} collective-permute-done((bf16[800,128]{1,0:T(8,128)(2,1)S(1)}, bf16[800,128]{1,0:T(8,128)(2,1)S(1)}, u32[]{:S(2)}, u32[]{:S(2)}) %collective-permute-start.8) | collective-permute-done | bytes 204832 | tf_op jit(solution)/shard_map/ppermute | solution.py:21
  106.5 6.4 %collective-permute-done.9 = bf16[800,128]{1,0:T(8,128)(2,1)S(1)} collective-permute-done((bf16[800,128]{1,0:T(8,128)(2,1)S(1)}, bf16[800,128]{1,0:T(8,128)(2,1)S(1)}, u32[]{:S(2)}, u32[]{:S(2)}) %collective-permute-start.9) | collective-permute-done | bytes 204832 | tf_op jit(solution)/shard_map/ppermute | solution.py:21
  112.9 6.4 %collective-permute-done.10 = bf16[800,128]{1,0:T(8,128)(2,1)S(1)} collective-permute-done((bf16[800,128]{1,0:T(8,128)(2,1)S(1)}, bf16[800,128]{1,0:T(8,128)(2,1)S(1)}, u32[]{:S(2)}, u32[]{:S(2)}) %collective-permute-start.10) | collective-permute-done | bytes 204832 | tf_op jit(solution)/shard_map/ppermute | solution.py:21
  119.3 6.4 %collective-permute-done.11 = bf16[800,128]{1,0:T(8,128)(2,1)S(1)} collective-permute-done((bf16[800,128]{1,0:T(8,128)(2,1)S(1)}, bf16[800,128]{1,0:T(8,128)(2,1)S(1)}, u32[]{:S(2)}, u32[]{:S(2)}) %collective-permute-start.11) | collective-permute-done | bytes 204832 | tf_op jit(solution)/shard_map/ppermute | solution.py:21
  125.7 6.4 %collective-permute-done.12 = bf16[800,128]{1,0:T(8,128)(2,1)S(1)} collective-permute-done((bf16[800,128]{1,0:T(8,128)(2,1)S(1)}, bf16[800,128]{1,0:T(8,128)(2,1)S(1)}, u32[]{:S(2)}, u32[]{:S(2)}) %collective-permute-start.12) | collective-permute-done | bytes 204832 | tf_op jit(solution)/shard_map/ppermute | solution.py:21
  132.1 6.4 %collective-permute-done.13 = bf16[800,128]{1,0:T(8,128)(2,1)S(1)} collective-permute-done((bf16[800,128]{1,0:T(8,128)(2,1)S(1)}, bf16[800,128]{1,0:T(8,128)(2,1)S(1)}, u32[]{:S(2)}, u32[]{:S(2)}) %collective-permute-start.13) | collective-permute-done | bytes 204832 | tf_op jit(solution)/shard_map/ppermute | solution.py:21
  138.5 6.4 %collective-permute-done.14 = bf16[800,128]{1,0:T(8,128)(2,1)S(1)} collective-permute-done((bf16[800,128]{1,0:T(8,128)(2,1)S(1)}, bf16[800,128]{1,0:T(8,128)(2,1)S(1)}, u32[]{:S(2)}, u32[]{:S(2)}) %collective-permute-start.14) | collective-permute-done | bytes 204832 | tf_op jit(solution)/shard_map/ppermute | solution.py:21
  144.9 2.7 gather_fusion.1
  147.6 13.6 %fusion = bf16[256,8,16,128]{3,1,2,0:T(8,128)(2,1)} fusion(bf16[800,2048]{1,0:T(8,128)(2,1)} %all-gather.2.cloned.1.call-done, bf16[16,800,128]{2,1,0:T(8,128)(2,1)} %gather_fusion.1), kind=kOutput, calls=%fused_computation.7 | convolution fusion | flops 6719275008 | bytes 14942208 | tf_op jit(solution)/shard_map/dot_general | solution.py:48
  161.3 9.7 %copy.26 = bf16[256,8,16,128]{3,2,1,0:T(8,128)(2,1)} copy(bf16[256,8,16,128]{3,1,2,0:T(8,128)(2,1)} %fusion) | data formatting | bytes 16777216
  171.0 9.1 %copy.32 = bf16[16,128,16,128]{3,1,2,0:T(8,128)(2,1)} copy(bf16[16,128,16,128]{3,2,1,0:T(8,128)(2,1)} %bitcast.77) | data formatting | bytes 16777216 | tf_op jit(solution)/shard_map/reshape | solution.py:56
  180.1 4.9 %gather_fusion.2 = bf16[96,128,128]{2,1,0:T(8,128)(2,1)S(1)} fusion(bf16[16,16,128,128]{3,2,1,0:T(8,128)(2,1)} %bitcast.78, s32[96]{0:T(128)S(1)} %reshape.372), kind=kCustom, calls=%fused_computation.2 | custom fusion | bytes 6292224 | tf_op jit(solution)/shard_map/gather | solution.py:83
  185.0 1.9 broadcast_select_fusion
  187.0 12.3 %all-to-all-start.1 = ((bf16[16,6,128,128]{3,2,1,0:T(8,128)(2,1)}), bf16[16,6,128,128]{3,2,1,0:T(8,128)(2,1)S(1)}, u32[]{:S(2)}, u32[]{:S(2)}) async-start(bf16[16,6,128,128]{3,2,1,0:T(8,128)(2,1)} %broadcast_select_fusion), calls=%async_computation.1 | async-start | bytes 6291456 | tf_op jit(solution)/shard_map/all_to_all | solution.py:87
  199.3 0.5 broadcast.429
  199.8 0.7 fusion.15
  200.8 0.6 slice.23
  201.5 0.2 select_reduce_fusion
  201.7 1.2 gather_fusion.4
  202.9 0.7 compare_and_fusion
  203.6 1.2 compare_select_fusion.9
  204.9 65.3 %all-to-all-done.1 = bf16[16,6,128,128]{3,2,1,0:T(8,128)(2,1)S(1)} async-done(((bf16[16,6,128,128]{3,2,1,0:T(8,128)(2,1)}), bf16[16,6,128,128]{3,2,1,0:T(8,128)(2,1)S(1)}, u32[]{:S(2)}, u32[]{:S(2)}) %all-to-all-start.1) | async-done | bytes 3145760 | tf_op jit(solution)/shard_map/all_to_all | solution.py:87
  270.2 2.7 gather_fusion.3
  272.9 3.4 %fusion.3 = bf16[1,1,96,128,128]{4,3,2,1,0:T(8,128)(2,1)} fusion(bf16[96,128,128]{2,1,0:T(8,128)(2,1)} %gather_fusion.3, pred[96]{0:T(512)(128)(4,1)S(1)} %get-tuple-element.10, pred[96]{0:T(512)(128)(4,1)S(1)} %get-tuple-element.11), kind=kLoop, calls=%fused_computation.11 | loop fusion | flops 3145728 | bytes 6291648 | tf_op jit(solution)/shard_map/jit(_where)/select_n | solution.py:36
  (55 shorter events, 1.6 us)
Async XLA Ops:
  7.2 7.7 %copy-start = (s32[16,16]{1,0:T(8,128)S(1)}, s32[16,16]{1,0:T(8,128)}, u32[]{:S(2)}) copy-start(s32[16,16]{1,0:T(8,128)} %param.4) | copy-start | bytes 3076
  7.2 140.4 %all-gather.2.cloned.1.call-start = ((), (), s32[]{:S(2)}) async-start(), calls=%async_computation.2 | async-start | bytes 3481600 | tf_op jit(solution)/shard_map/all_gather | solution.py:47
  11.3 49.0 %collective-permute-start = (bf16[800,128]{1,0:T(8,128)(2,1)}, bf16[800,128]{1,0:T(8,128)(2,1)S(1)}, u32[]{:S(2)}, u32[]{:S(2)}) collective-permute-start(bf16[800,128]{1,0:T(8,128)(2,1)} %get-tuple-element.7), channel_id=1, source_target_pairs={{0,16},{16,32},{32,48},{48,64},{64,80},{80,96},{96,112},{112,128},... | collective-permute-start | bytes 614408 | tf_op jit(solution)/shard_map/ppermute | solution.py:21
  17.0 170.0 %all-to-all-start = ((s32[16,1,6]{2,1,0:T(1,128)}), s32[16,1,6]{2,1,0:T(1,128)S(1)}, u32[]{:S(2)}, u32[]{:S(2)}) async-start(s32[16,1,6]{2,1,0:T(1,128)} %copy.20), calls=%async_computation | async-start | bytes 16384 | tf_op jit(solution)/shard_map/all_to_all | solution.py:88
  60.3 4.4 %collective-permute-start.1 = (bf16[800,128]{1,0:T(8,128)(2,1)S(1)}, bf16[800,128]{1,0:T(8,128)(2,1)S(1)}, u32[]{:S(2)}, u32[]{:S(2)}) collective-permute-start(bf16[800,128]{1,0:T(8,128)(2,1)S(1)} %collective-permute-done), channel_id=1, source_target_pairs={{0,16},{16,32},{32,48},{48,64},{64,80},{80,96},{96,112},{112,128},... | collective-permute-start | bytes 614408 | tf_op jit(solution)/shard_map/ppermute | solution.py:21
  64.8 5.2 %collective-permute-start.2 = (bf16[800,128]{1,0:T(8,128)(2,1)S(1)}, bf16[800,128]{1,0:T(8,128)(2,1)S(1)}, u32[]{:S(2)}, u32[]{:S(2)}) collective-permute-start(bf16[800,128]{1,0:T(8,128)(2,1)S(1)} %collective-permute-done.1), channel_id=1, source_target_pairs={{0,16},{16,32},{32,48},{48,64},{64,80},{80,96},{96,112},{112,128},... | collective-permute-start | bytes 614408 | tf_op jit(solution)/shard_map/ppermute | solution.py:21
  70.0 5.2 %collective-permute-start.3 = (bf16[800,128]{1,0:T(8,128)(2,1)S(1)}, bf16[800,128]{1,0:T(8,128)(2,1)S(1)}, u32[]{:S(2)}, u32[]{:S(2)}) collective-permute-start(bf16[800,128]{1,0:T(8,128)(2,1)S(1)} %collective-permute-done.2), channel_id=1, source_target_pairs={{0,16},{16,32},{32,48},{48,64},{64,80},{80,96},{96,112},{112,128},... | collective-permute-start | bytes 614408 | tf_op jit(solution)/shard_map/ppermute | solution.py:21
  75.1 5.8 %collective-permute-start.4 = (bf16[800,128]{1,0:T(8,128)(2,1)S(1)}, bf16[800,128]{1,0:T(8,128)(2,1)S(1)}, u32[]{:S(2)}, u32[]{:S(2)}) collective-permute-start(bf16[800,128]{1,0:T(8,128)(2,1)S(1)} %collective-permute-done.3), channel_id=1, source_target_pairs={{0,16},{16,32},{32,48},{48,64},{64,80},{80,96},{96,112},{112,128},... | collective-permute-start | bytes 614408 | tf_op jit(solution)/shard_map/ppermute | solution.py:21
  80.9 6.4 %collective-permute-start.5 = (bf16[800,128]{1,0:T(8,128)(2,1)S(1)}, bf16[800,128]{1,0:T(8,128)(2,1)S(1)}, u32[]{:S(2)}, u32[]{:S(2)}) collective-permute-start(bf16[800,128]{1,0:T(8,128)(2,1)S(1)} %collective-permute-done.4), channel_id=1, source_target_pairs={{0,16},{16,32},{32,48},{48,64},{64,80},{80,96},{96,112},{112,128},... | collective-permute-start | bytes 614408 | tf_op jit(solution)/shard_map/ppermute | solution.py:21
  87.3 6.4 %collective-permute-start.6 = (bf16[800,128]{1,0:T(8,128)(2,1)S(1)}, bf16[800,128]{1,0:T(8,128)(2,1)S(1)}, u32[]{:S(2)}, u32[]{:S(2)}) collective-permute-start(bf16[800,128]{1,0:T(8,128)(2,1)S(1)} %collective-permute-done.5), channel_id=1, source_target_pairs={{0,16},{16,32},{32,48},{48,64},{64,80},{80,96},{96,112},{112,128},... | collective-permute-start | bytes 614408 | tf_op jit(solution)/shard_map/ppermute | solution.py:21
  93.7 6.4 %collective-permute-start.7 = (bf16[800,128]{1,0:T(8,128)(2,1)S(1)}, bf16[800,128]{1,0:T(8,128)(2,1)S(1)}, u32[]{:S(2)}, u32[]{:S(2)}) collective-permute-start(bf16[800,128]{1,0:T(8,128)(2,1)S(1)} %collective-permute-done.6), channel_id=1, source_target_pairs={{0,16},{16,32},{32,48},{48,64},{64,80},{80,96},{96,112},{112,128},... | collective-permute-start | bytes 614408 | tf_op jit(solution)/shard_map/ppermute | solution.py:21
  100.1 6.4 %collective-permute-start.8 = (bf16[800,128]{1,0:T(8,128)(2,1)S(1)}, bf16[800,128]{1,0:T(8,128)(2,1)S(1)}, u32[]{:S(2)}, u32[]{:S(2)}) collective-permute-start(bf16[800,128]{1,0:T(8,128)(2,1)S(1)} %collective-permute-done.7), channel_id=1, source_target_pairs={{0,16},{16,32},{32,48},{48,64},{64,80},{80,96},{96,112},{112,128},... | collective-permute-start | bytes 614408 | tf_op jit(solution)/shard_map/ppermute | solution.py:21
  106.5 6.4 %collective-permute-start.9 = (bf16[800,128]{1,0:T(8,128)(2,1)S(1)}, bf16[800,128]{1,0:T(8,128)(2,1)S(1)}, u32[]{:S(2)}, u32[]{:S(2)}) collective-permute-start(bf16[800,128]{1,0:T(8,128)(2,1)S(1)} %collective-permute-done.8), channel_id=1, source_target_pairs={{0,16},{16,32},{32,48},{48,64},{64,80},{80,96},{96,112},{112,128},... | collective-permute-start | bytes 614408 | tf_op jit(solution)/shard_map/ppermute | solution.py:21
  112.9 6.4 %collective-permute-start.10 = (bf16[800,128]{1,0:T(8,128)(2,1)S(1)}, bf16[800,128]{1,0:T(8,128)(2,1)S(1)}, u32[]{:S(2)}, u32[]{:S(2)}) collective-permute-start(bf16[800,128]{1,0:T(8,128)(2,1)S(1)} %collective-permute-done.9), channel_id=1, source_target_pairs={{0,16},{16,32},{32,48},{48,64},{64,80},{80,96},{96,112},{112,128},... | collective-permute-start | bytes 614408 | tf_op jit(solution)/shard_map/ppermute | solution.py:21
  119.3 6.4 %collective-permute-start.11 = (bf16[800,128]{1,0:T(8,128)(2,1)S(1)}, bf16[800,128]{1,0:T(8,128)(2,1)S(1)}, u32[]{:S(2)}, u32[]{:S(2)}) collective-permute-start(bf16[800,128]{1,0:T(8,128)(2,1)S(1)} %collective-permute-done.10), channel_id=1, source_target_pairs={{0,16},{16,32},{32,48},{48,64},{64,80},{80,96},{96,112},{112,128},... | collective-permute-start | bytes 614408 | tf_op jit(solution)/shard_map/ppermute | solution.py:21
  125.7 6.4 %collective-permute-start.12 = (bf16[800,128]{1,0:T(8,128)(2,1)S(1)}, bf16[800,128]{1,0:T(8,128)(2,1)S(1)}, u32[]{:S(2)}, u32[]{:S(2)}) collective-permute-start(bf16[800,128]{1,0:T(8,128)(2,1)S(1)} %collective-permute-done.11), channel_id=1, source_target_pairs={{0,16},{16,32},{32,48},{48,64},{64,80},{80,96},{96,112},{112,128},... | collective-permute-start | bytes 614408 | tf_op jit(solution)/shard_map/ppermute | solution.py:21
  132.1 6.4 %collective-permute-start.13 = (bf16[800,128]{1,0:T(8,128)(2,1)S(1)}, bf16[800,128]{1,0:T(8,128)(2,1)S(1)}, u32[]{:S(2)}, u32[]{:S(2)}) collective-permute-start(bf16[800,128]{1,0:T(8,128)(2,1)S(1)} %collective-permute-done.12), channel_id=1, source_target_pairs={{0,16},{16,32},{32,48},{48,64},{64,80},{80,96},{96,112},{112,128},... | collective-permute-start | bytes 614408 | tf_op jit(solution)/shard_map/ppermute | solution.py:21
  138.5 6.4 %collective-permute-start.14 = (bf16[800,128]{1,0:T(8,128)(2,1)S(1)}, bf16[800,128]{1,0:T(8,128)(2,1)S(1)}, u32[]{:S(2)}, u32[]{:S(2)}) collective-permute-start(bf16[800,128]{1,0:T(8,128)(2,1)S(1)} %collective-permute-done.13), channel_id=1, source_target_pairs={{0,16},{16,32},{32,48},{48,64},{64,80},{80,96},{96,112},{112,128},... | collective-permute-start | bytes 614408 | tf_op jit(solution)/shard_map/ppermute | solution.py:21
  187.0 83.2 %all-to-all-start.1 = ((bf16[16,6,128,128]{3,2,1,0:T(8,128)(2,1)}), bf16[16,6,128,128]{3,2,1,0:T(8,128)(2,1)S(1)}, u32[]{:S(2)}, u32[]{:S(2)}) async-start(bf16[16,6,128,128]{3,2,1,0:T(8,128)(2,1)} %broadcast_select_fusion), calls=%async_computation.1 | async-start | bytes 6291456 | tf_op jit(solution)/shard_map/all_to_all | solution.py:87
Sparse Core Ops, SparseCore 0:
  11.4 113.1 all-gather.1
